TPU v7x, 512 devices: a whole 4x4x16 slice. The times are simulated.
512 devices in a mesh: lat: 128 (over y, z, x_hi), lon: 4 (over x_lo, core).
Axes of the slice: x: 4 (x_hi: 2, x_lo: 2; x = x_hi * 2 + x_lo), y: 4, z: 16, core: 2. Of those that a mesh axis runs over, the one named last changes fastest.
Arguments:
- grid_state: bfloat16 [256, 720, 640], P('lat', 'lon'), may hold values from -6 to 6
- conv_weight: float32 [3, 3, 640], replicated, may hold values from -2.4 to 2.4
- spectral_gain: float32 [2, 256, 640], P(None, None, 'lon'), may hold values from -4 to 4
- spectral_weight: bfloat16 [2, 640, 640], P(None, None, 'lon'), may hold values from -0.125 to 0.125
- norm_gain: float32 [640], replicated, may hold values from 0.1 to 1.9
- expand_weight: bfloat16 [640, 1280], replicated, may hold values from -0.25 to 0.25
- reduce_weight: bfloat16 [1280, 640], replicated, may hold values from -0.15625 to 0.15625
Outputs:
- block_output: bfloat16 [256, 720, 640], P('lat', 'lon')
All inputs are finite; a program needn't handle non-finite values.
Results may differ from a plain program's by a relative error of at most 0.015.
Values may be sent and summed in bfloat16 or wider, within the bound.
A program may use at most 64 MiB of HBM per device.

v0:
```python
import math
import jax
import jax.numpy as jnp
from jax import lax
from jax.sharding import PartitionSpec as P

M = 256
norm_eps = 1e-06
underflow_cut = -60.0
degree_block = 16


def padded_2(value, sides, width, wrap):
    for axis, dim in sides:
        count, length = (lax.axis_size(axis), value.shape[dim])
        up = [(i, (i + 1) % count) for i in range(count if wrap else count - 1)]
        down = [(j, i) for i, j in up]
        last = lax.slice_in_dim(value, length - width, length, axis=dim)
        initial = lax.slice_in_dim(value, 0, width, axis=dim)
        before = lax.ppermute(last, axis, up)
        after = lax.ppermute(initial, axis, down)
        value = jnp.concatenate([before, value, after], axis=dim)
    return value


def joined_along(parts, dim):
    parts = jnp.moveaxis(parts, 0, dim)
    dims = parts.shape
    return parts.reshape(*dims[:dim], dims[dim] * dims[dim + 1], *dims[dim + 2 :])


def from_everyone(value, axis):
    copies = jnp.broadcast_to(value, (lax.axis_size(axis), *value.shape))
    return lax.all_to_all(copies, axis, split_axis=0, concat_axis=0, tiled=True)


def gathered_copies(value, axis, dim):
    return joined_along(from_everyone(value, axis), dim)


def legendre_table(orders, lat_total, degree_count):
    colatitude = (jnp.arange(lat_total, dtype=jnp.float32) + 0.5) * (math.pi / lat_total)
    cosines = jnp.cos(colatitude)
    sine_values = jnp.sin(colatitude)
    rank_values = jnp.arange(1, degree_count + 1, dtype=jnp.int32)
    rank_float = rank_values.astype(jnp.float32)
    log_terms = 0.5 * jnp.log((2.0 * rank_float + 1.0) / (2.0 * rank_float))
    log_norm = jnp.sum(
        jnp.where(rank_values[None, :] <= orders[:, None], log_terms[None, :], jnp.float32(0.0)),
        axis=1,
    )
    order_float = orders.astype(jnp.float32)[:, None]
    log_start = (
        -0.5 * math.log(4.0 * math.pi)
        + log_norm[:, None]
        + order_float * jnp.log(sine_values)[None, :]
    )
    start_value = jnp.where(
        log_start > underflow_cut, jnp.exp(jnp.maximum(log_start, underflow_cut)), jnp.float32(0.0)
    )

    def advance_block(totals, block_start):
        previous, earlier = totals
        rows_out = []
        for inner in range(degree_block):
            degree = block_start + inner
            degree_float = degree.astype(jnp.float32)
            raise_coef = jnp.sqrt(
                jnp.maximum(4.0 * degree_float * degree_float - 1.0, 0.0)
                / jnp.maximum(degree_float * degree_float - order_float * order_float, 1.0)
            )
            lower_coef = jnp.sqrt(
                jnp.maximum((degree_float - 1.0) ** 2 - order_float * order_float, 0.0)
                / jnp.maximum(4.0 * (degree_float - 1.0) ** 2 - 1.0, 1.0)
            )
            recurred = raise_coef * (cosines[None, :] * previous - lower_coef * earlier)
            current = jnp.where(
                degree < orders[:, None],
                jnp.float32(0.0),
                jnp.where(degree == orders[:, None], start_value, recurred),
            )
            earlier = previous
            previous = current
            rows_out.append(current)
        return ((previous, earlier), jnp.stack(rows_out, axis=0))

    blank = jnp.zeros((orders.shape[0], lat_total), jnp.float32)
    starts = jnp.arange(0, degree_count, degree_block, dtype=jnp.int32)
    unused, table_blocks = lax.scan(advance_block, (blank, blank), starts)
    return table_blocks.reshape(degree_count, orders.shape[0], lat_total)


def quadrature(lat_total):
    colatitude = (jnp.arange(lat_total, dtype=jnp.float32) + 0.5) * (math.pi / lat_total)
    return 2.0 * math.pi * math.pi / lat_total * jnp.sin(colatitude)


def fourier_table(longitudes, lon_total, mode_count):
    mode_index = jnp.arange(mode_count, dtype=jnp.int32)
    phase_index = longitudes[:, None] * mode_index[None, :] % lon_total
    angles = phase_index.astype(jnp.float32) * (2.0 * math.pi / lon_total)
    return (jnp.stack([jnp.cos(angles), -jnp.sin(angles)], axis=1) / lon_total).astype(jnp.bfloat16)


def synthesis_table(longitudes, lon_total, mode_count):
    mode_index = jnp.arange(mode_count, dtype=jnp.int32)
    phase_index = mode_index[:, None] * longitudes[None, :] % lon_total
    angles = phase_index.astype(jnp.float32) * (2.0 * math.pi / lon_total)
    doubling = jnp.where(mode_index == 0, 1.0, 2.0).astype(jnp.float32)[:, None]
    return jnp.stack([doubling * jnp.cos(angles), -doubling * jnp.sin(angles)], axis=0).astype(
        jnp.bfloat16
    )


def shards(
    grid_state, conv_weight, spectral_gain, spectral_weight, norm_gain, expand_weight, reduce_weight
):
    lat_rows, sector_width, channel_total = grid_state.shape
    lat_count = lax.axis_size("lat")
    lon_count = lax.axis_size("lon")
    lat_total = lat_rows * lat_count
    lon_total = sector_width * lon_count
    mode_count = M
    order_share = mode_count // lat_count
    channel_share = channel_total // lon_count
    lat_position = lax.axis_index("lat")
    wrapped = padded_2(grid_state, (("lon", 1),), 1, True)
    padded = padded_2(wrapped, (("lat", 0),), 1, False)
    padded_wide = padded.astype(jnp.float32)
    filtered = jnp.zeros((lat_rows, sector_width, channel_total), jnp.float32)
    for row_shift in range(3):
        for col_shift in range(3):
            filtered = (
                filtered
                + conv_weight[row_shift, col_shift]
                * padded_wide[
                    row_shift : row_shift + lat_rows, col_shift : col_shift + sector_width
                ]
            )
    first_section = (grid_state.astype(jnp.float32) + jax.nn.gelu(filtered)).astype(jnp.bfloat16)
    gathered = lax.all_to_all(first_section, "lon", split_axis=2, concat_axis=1, tiled=True)
    forward_table = fourier_table(jnp.arange(lon_total, dtype=jnp.int32), lon_total, mode_count)
    spectrum = jnp.einsum(
        "tpc,prm->tmrc", gathered, forward_table, preferred_element_type=jnp.float32
    ).astype(jnp.bfloat16)
    cycle_spectrum = lax.all_to_all(spectrum, "lat", split_axis=1, concat_axis=0, tiled=True)
    orders = lat_position * order_share + jnp.arange(order_share, dtype=jnp.int32)
    legendre = legendre_table(orders, lat_total, mode_count)
    analysis_table = (legendre * quadrature(lat_total)[None, None, :]).astype(jnp.bfloat16)
    coefficients = jnp.einsum(
        "lmt,tmrc->lmrc", analysis_table, cycle_spectrum, preferred_element_type=jnp.float32
    )
    gain_real = spectral_gain[0][:, None, :]
    gain_imag = spectral_gain[1][:, None, :]
    coef_real = coefficients[:, :, 0, :]
    coef_imag = coefficients[:, :, 1, :]
    gained = jnp.stack(
        [
            gain_real * coef_real - gain_imag * coef_imag,
            gain_real * coef_imag + gain_imag * coef_real,
        ],
        axis=2,
    ).astype(jnp.bfloat16)
    blank = jnp.zeros((mode_count * order_share, channel_share), jnp.float32)
    portion = gathered_copies(gained, "lon", 3)
    width_part = portion.shape[3]
    weight_rows = lax.slice_in_dim(spectral_weight, 0, width_part, axis=1)
    real_part = portion[:, :, 0, :].reshape(-1, width_part)
    imag_part = portion[:, :, 1, :].reshape(-1, width_part)
    real_sum = (
        blank
        + jnp.dot(real_part, weight_rows[0], preferred_element_type=jnp.float32)
        - jnp.dot(imag_part, weight_rows[1], preferred_element_type=jnp.float32)
    )
    imag_sum = (
        blank
        + jnp.dot(real_part, weight_rows[1], preferred_element_type=jnp.float32)
        + jnp.dot(imag_part, weight_rows[0], preferred_element_type=jnp.float32)
    )
    mixed = jnp.stack(
        [
            real_sum.reshape(mode_count, order_share, channel_share),
            imag_sum.reshape(mode_count, order_share, channel_share),
        ],
        axis=2,
    ).astype(jnp.bfloat16)
    synthesis_legendre = legendre.astype(jnp.bfloat16)
    cycle_modes = jnp.einsum(
        "lmt,lmrc->tmrc", synthesis_legendre, mixed, preferred_element_type=jnp.float32
    ).astype(jnp.bfloat16)
    band_modes = lax.all_to_all(cycle_modes, "lat", split_axis=0, concat_axis=1, tiled=True)
    inverse_table = synthesis_table(jnp.arange(lon_total, dtype=jnp.int32), lon_total, mode_count)
    all_lons = jnp.einsum(
        "tmrc,rmp->tpc", band_modes, inverse_table, preferred_element_type=jnp.float32
    )
    spectral_out = lax.all_to_all(
        all_lons.astype(jnp.bfloat16), "lon", split_axis=1, concat_axis=2, tiled=True
    ).astype(all_lons.dtype)
    second_section = (first_section.astype(jnp.float32) + spectral_out).astype(jnp.bfloat16)
    second_wide = second_section.astype(jnp.float32)
    scale_values = lax.rsqrt(jnp.mean(second_wide * second_wide, axis=-1, keepdims=True) + norm_eps)
    normed = (second_wide * norm_gain * scale_values).astype(jnp.bfloat16)
    flat_rows = normed.reshape(-1, channel_total)
    hidden = jax.nn.gelu(
        jnp.dot(flat_rows, expand_weight, preferred_element_type=jnp.float32)
    ).astype(jnp.bfloat16)
    update = jnp.dot(hidden, reduce_weight, preferred_element_type=jnp.float32)
    block_output = (second_wide.reshape(-1, channel_total) + update).astype(jnp.bfloat16)
    return block_output.reshape(lat_rows, sector_width, channel_total)


def solution(mesh):
    return jax.shard_map(
        shards,
        mesh=mesh,
        in_specs=(
            P("lat", "lon", None),
            P(),
            P(None, None, "lon"),
            P(None, None, "lon"),
            P(),
            P(),
            P(),
        ),
        out_specs=P("lat", "lon", None),
        check_vma=False,
    )
```

profile of v0, /device:TPU:1, one launch (start us, length us, event | category | flops | bytes accessed | tf_op | source)
XLA Modules:
  0.0 384.5 jit_solution(18043150537942124979)
XLA Ops:
  0.0 1.2 copy.66
  1.2 4.5 %collective-permute-start = (bf16[2,1,640]{2,1,0:T(2,128)(2,1)S(1)}, bf16[2,1,640]{2,1,0:T(2,128)(2,1)S(1)}, u32[]{:S(2)}, u32[]{:S(2)}) collective-permute-start(bf16[2,1,640]{2,1,0:T(2,128)(2,1)S(1)} %get-tuple-element.533), channel_id=1, source_target_pairs={{0,1},{1,2},{2,3},{3,0},{4,5},{5,6},{6,7},{7,4},{8,9},{9,10},{10,1... | collective-permute-start | bytes 7688 | tf_op jit(solution)/shard_map/ppermute | solution.py:20
  5.7 6.2 %collective-permute-start.1 = (bf16[2,1,640]{2,1,0:T(2,128)(2,1)S(1)}, bf16[2,1,640]{2,1,0:T(2,128)(2,1)S(1)}, u32[]{:S(2)}, u32[]{:S(2)}) collective-permute-start(bf16[2,1,640]{2,1,0:T(2,128)(2,1)S(1)} %get-tuple-element.534), channel_id=1, source_target_pairs={{1,0},{2,1},{3,2},{0,3},{5,4},{6,5},{7,6},{4,7},{9,8},{10,9},{11,1... | collective-permute-start | bytes 7688 | tf_op jit(solution)/shard_map/ppermute | solution.py:21
  11.9 0.9 slice_reduce_fusion.8
  13.1 2.1 collective-permute-start.2
  15.2 1.3 collective-permute-start.3
  16.5 4.3 %sine_negate_fusion = (f32[720,1,256]{2,0,1:T(8,128)}, f32[720,1,256]{2,0,1:T(8,128)}) fusion(), kind=kLoop, calls=%fused_computation.182 | loop fusion | flops 1843200 | bytes 1474560 | tf_op jit(solution)/shard_map/neg | solution.py:102
  20.8 3.9 %collective-permute-done.3 = bf16[1,182,640]{2,1,0:T(8,128)(2,1)S(1)} collective-permute-done((bf16[1,182,640]{2,1,0:T(8,128)(2,1)S(1)}, bf16[1,182,640]{2,1,0:T(8,128)(2,1)S(1)}, u32[]{:S(2)}, u32[]{:S(2)}) %collective-permute-start.3) | collective-permute-done | bytes 232992 | tf_op jit(solution)/shard_map/ppermute | solution.py:21
  24.8 1.1 fusion.67
  26.0 1.8 copy.70
  27.7 10.6 %all-to-all-start = ((bf16[2,180,640]{1,0,2:T(2,128)(2,1)}), bf16[2,180,640]{1,0,2:T(2,128)(2,1)S(1)}, u32[]{:S(2)}, u32[]{:S(2)}) async-start(bf16[2,180,640]{1,0,2:T(2,128)(2,1)} %copy.70), calls=%async_computation | async-start | bytes 1310720 | tf_op jit(solution)/shard_map/all_to_all | solution.py:141
  38.5 9.1 %all-to-all-done = bf16[2,180,640]{1,0,2:T(2,128)(2,1)S(1)} async-done(((bf16[2,180,640]{1,0,2:T(2,128)(2,1)}), bf16[2,180,640]{1,0,2:T(2,128)(2,1)S(1)}, u32[]{:S(2)}, u32[]{:S(2)}) %all-to-all-start) | async-done | bytes 460832 | tf_op jit(solution)/shard_map/all_to_all | solution.py:141
  48.6 1.8 fusion.56
  50.4 1.2 copy.73
  51.5 16.9 %all-to-all-start.1 = ((bf16[2,256,2,160]{3,0,2,1:T(2,128)(2,1)}), bf16[2,256,2,160]{3,0,2,1:T(2,128)(2,1)S(1)}, u32[]{:S(2)}, u32[]{:S(2)}) async-start(bf16[2,256,2,160]{3,0,2,1:T(2,128)(2,1)} %copy.73), calls=%async_computation.1 | async-start | bytes 1048576 | tf_op jit(solution)/shard_map/all_to_all | solution.py:146
  68.4 201.7 %while.21 = (s32[]{:T(128)}, f32[2,256]{1,0:T(2,128)S(1)}, f32[2,256]{1,0:T(2,128)S(1)}, f32[16,16,2,256]{3,2,1,0:T(2,128)S(1)}, s32[16]{0:T(128)S(1)}, /*index=...) while((s32[]{:T(128)}, f32[2,256]{1,0:T(2,128)S(1)}, ...), condition=%wide.region_2.3_spmd.clone.clone.clone.clone, body=%wide.region_1.2_spmd.clone.clone.clone.clone.sunk | while | flops 92737 | bytes 279792 | solution.py:89
  68.4 0.6 dynamic_slice.13
  70.2 0.6 fusion.163
  81.0 0.6 dynamic_slice.13
  82.8 0.6 fusion.163
  93.7 0.6 dynamic_slice.13
  95.4 0.6 fusion.163
  106.3 0.6 dynamic_slice.13
  118.9 0.6 dynamic_slice.13
  131.5 0.6 dynamic_slice.13
  133.3 0.6 fusion.163
  144.1 0.6 dynamic_slice.13
  145.9 0.6 fusion.163
  156.7 0.6 dynamic_slice.13
  158.5 0.6 fusion.163
  169.3 0.6 dynamic_slice.13
  181.9 0.6 dynamic_slice.13
  194.5 0.6 dynamic_slice.13
  207.1 0.6 dynamic_slice.13
  208.9 0.6 fusion.163
  219.7 0.6 dynamic_slice.13
  221.5 0.6 fusion.163
  232.3 0.6 dynamic_slice.13
  234.1 0.6 fusion.163
  244.9 0.6 dynamic_slice.13
  246.7 0.6 fusion.163
  257.5 0.6 dynamic_slice.13
  271.3 19.9 %all_to_all.68 = bf16[4,256,2,2,160]{1,4,3,2,0:T(8,128)(2,1)S(1)} all-to-all(bf16[4,256,2,2,160]{1,4,3,2,0:T(8,128)(2,1)S(1)} %broadcast_in_dim.453), channel_id=1, replica_groups=mesh['lat'=128,'lon'=4] {'lon'}, dimensions={0} | all-to-all | bytes 2621440 | tf_op jit(solution)/shard_map/all_to_all | solution.py:34
  291.4 1.8 copy.79
  293.2 2.1 reshape_squeeze.6
  295.3 1.1 fusion.112
  296.4 1.1 fusion.108
  297.5 1.1 copy.80
  298.9 1.4 fusion.57
  300.4 0.8 stack_reshape.8
  301.2 1.1 copy.83
  303.2 1.3 fusion.55
  304.5 1.2 copy.86
  305.6 18.3 %all-to-all-start.3 = ((bf16[256,2,2,160]{3,2,1,0:T(2,128)(2,1)}), bf16[256,2,2,160]{3,2,1,0:T(2,128)(2,1)S(1)}, u32[]{:S(2)}, u32[]{:S(2)}) async-start(bf16[256,2,2,160]{3,2,1,0:T(2,128)(2,1)} %copy.86), calls=%async_computation.3 | async-start | bytes 1048576 | tf_op jit(solution)/shard_map/all_to_all | solution.py:191
  324.0 4.1 %multiply_convert_fusion.1 = (bf16[1,256,720]{1,2,0:T(8,128)(2,1)S(1)}, bf16[1,256,720]{1,2,0:T(8,128)(2,1)}) fusion(f32[256]{0:T(256)S(1)} %fusion.123, f32[256]{0:T(256)S(1)} %compare_select_fusion.2), kind=kLoop, calls=%fused_computation.187 | loop fusion | flops 2396160 | bytes 739328 | tf_op jit(solution)/shard_map/convert.10
  328.1 27.1 %all-to-all-done.3 = bf16[256,2,2,160]{3,2,1,0:T(2,128)(2,1)S(1)} async-done(((bf16[256,2,2,160]{3,2,1,0:T(2,128)(2,1)}), bf16[256,2,2,160]{3,2,1,0:T(2,128)(2,1)S(1)}, u32[]{:S(2)}, u32[]{:S(2)}) %all-to-all-start.3) | async-done | bytes 327712 | tf_op jit(solution)/shard_map/all_to_all | solution.py:191
  355.5 1.5 fusion.54
  357.0 1.0 copy.89
  358.0 16.8 %all_to_all.69 = bf16[2,720,160]{2,0,1:T(2,128)(2,1)S(1)} all-to-all(bf16[2,720,160]{2,0,1:T(2,128)(2,1)S(1)} %copy.89), channel_id=1, replica_groups=mesh['lat'=128,'lon'=4] {'lon'}, dimensions={1} | all-to-all | bytes 921600 | tf_op jit(solution)/shard_map/all_to_all | solution.py:196
  375.1 1.9 reshape.1013
  377.0 1.5 multiply_reduce_fusion
  378.6 1.0 reshape.1010
  379.8 3.4 fusion.53
  383.4 1.1 copy.91
  (851 shorter events, 38.1 us)
Async XLA Ops:
  0.0 379.8 %copy-start = (bf16[1280,640]{1,0:T(8,128)(2,1)S(1)}, bf16[1280,640]{1,0:T(8,128)(2,1)}, u32[]{:S(2)}) copy-start(bf16[1280,640]{1,0:T(8,128)(2,1)} %param.15) | copy-start | bytes 4915204
  1.2 11.7 %collective-permute-start = (bf16[2,1,640]{2,1,0:T(2,128)(2,1)S(1)}, bf16[2,1,640]{2,1,0:T(2,128)(2,1)S(1)}, u32[]{:S(2)}, u32[]{:S(2)}) collective-permute-start(bf16[2,1,640]{2,1,0:T(2,128)(2,1)S(1)} %get-tuple-element.533), channel_id=1, source_target_pairs={{0,1},{1,2},{2,3},{3,0},{4,5},{5,6},{6,7},{7,4},{8,9},{9,10},{10,1... | collective-permute-start | bytes 7688 | tf_op jit(solution)/shard_map/ppermute | solution.py:20
  5.7 7.2 %collective-permute-start.1 = (bf16[2,1,640]{2,1,0:T(2,128)(2,1)S(1)}, bf16[2,1,640]{2,1,0:T(2,128)(2,1)S(1)}, u32[]{:S(2)}, u32[]{:S(2)}) collective-permute-start(bf16[2,1,640]{2,1,0:T(2,128)(2,1)S(1)} %get-tuple-element.534), channel_id=1, source_target_pairs={{1,0},{2,1},{3,2},{0,3},{5,4},{6,5},{7,6},{4,7},{9,8},{10,9},{11,1... | collective-permute-start | bytes 7688 | tf_op jit(solution)/shard_map/ppermute | solution.py:21
  13.1 7.7 %collective-permute-start.2 = (bf16[1,182,640]{2,1,0:T(8,128)(2,1)S(1)}, bf16[1,182,640]{2,1,0:T(8,128)(2,1)S(1)}, u32[]{:S(2)}, u32[]{:S(2)}) collective-permute-start(bf16[1,182,640]{2,1,0:T(8,128)(2,1)S(1)} %get-tuple-element.531), channel_id=1, source_target_pairs={{0,4},{4,8},{8,12},{12,16},{16,20},{20,24},{24,28},{28,32},{32,36}... | collective-permute-start | bytes 698888 | tf_op jit(solution)/shard_map/ppermute | solution.py:20
  15.2 9.5 %collective-permute-start.3 = (bf16[1,182,640]{2,1,0:T(8,128)(2,1)S(1)}, bf16[1,182,640]{2,1,0:T(8,128)(2,1)S(1)}, u32[]{:S(2)}, u32[]{:S(2)}) collective-permute-start(bf16[1,182,640]{2,1,0:T(8,128)(2,1)S(1)} %get-tuple-element.532), channel_id=1, source_target_pairs={{4,0},{8,4},{12,8},{16,12},{20,16},{24,20},{28,24},{32,28},{36,32}... | collective-permute-start | bytes 698888 | tf_op jit(solution)/shard_map/ppermute | solution.py:21
  16.5 8.3 %copy-start.2 = (bf16[2,180,640]{2,0,1:T(2,128)(2,1)S(1)}, bf16[2,180,640]{2,0,1:T(2,128)(2,1)}, u32[]{:S(2)}) copy-start(bf16[2,180,640]{2,0,1:T(2,128)(2,1)} %param.9) | copy-start | bytes 1382404
  25.9 22.1 %copy-start.1 = (bf16[2,180,640]{2,1,0:T(8,128)(2,1)}, bf16[2,180,640]{2,1,0:T(8,128)(2,1)S(1)}, u32[]{:S(2)}) copy-start(bf16[2,180,640]{2,1,0:T(8,128)(2,1)S(1)} %fusion.67) | copy-start | bytes 1382404
  27.7 19.8 %all-to-all-start = ((bf16[2,180,640]{1,0,2:T(2,128)(2,1)}), bf16[2,180,640]{1,0,2:T(2,128)(2,1)S(1)}, u32[]{:S(2)}, u32[]{:S(2)}) async-start(bf16[2,180,640]{1,0,2:T(2,128)(2,1)} %copy.70), calls=%async_computation | async-start | bytes 1310720 | tf_op jit(solution)/shard_map/all_to_all | solution.py:141
  48.5 19.9 %copy-start.5 = (f32[16,16,2,256]{3,2,1,0:T(2,128)S(1)}, f32[16,16,2,256]{3,2,1,0:T(2,128)}, u32[]{:S(2)}) copy-start(f32[16,16,2,256]{3,2,1,0:T(2,128)} %custom-call.3) | copy-start | bytes 1572868
  51.5 218.7 %all-to-all-start.1 = ((bf16[2,256,2,160]{3,0,2,1:T(2,128)(2,1)}), bf16[2,256,2,160]{3,0,2,1:T(2,128)(2,1)S(1)}, u32[]{:S(2)}, u32[]{:S(2)}) async-start(bf16[2,256,2,160]{3,0,2,1:T(2,128)(2,1)} %copy.73), calls=%async_computation.1 | async-start | bytes 1048576 | tf_op jit(solution)/shard_map/all_to_all | solution.py:146
  68.4 201.8 %copy-start.7 = (f32[2,256,160]{1,2,0:T(8,128)S(1)}, f32[2,256,160]{1,2,0:T(8,128)}, u32[]{:S(2)}) copy-start(f32[2,256,160]{1,2,0:T(8,128)} %param.11) | copy-start | bytes 983044
  270.1 1.0 copy-start.6
  291.3 3.9 %copy-start.3 = (bf16[2,640,160]{1,2,0:T(8,128)(2,1)S(1)}, bf16[2,640,160]{1,2,0:T(8,128)(2,1)}, u32[]{:S(2)}) copy-start(bf16[2,640,160]{1,2,0:T(8,128)(2,1)} %param.12) | copy-start | bytes 1228804
  298.8 3.5 copy-start.4
  305.6 49.5 %all-to-all-start.3 = ((bf16[256,2,2,160]{3,2,1,0:T(2,128)(2,1)}), bf16[256,2,2,160]{3,2,1,0:T(2,128)(2,1)S(1)}, u32[]{:S(2)}, u32[]{:S(2)}) async-start(bf16[256,2,2,160]{3,2,1,0:T(2,128)(2,1)} %copy.86), calls=%async_computation.3 | async-start | bytes 1048576 | tf_op jit(solution)/shard_map/all_to_all | solution.py:191
  377.0 2.6 copy-start.8
where the time goes:
time: 387 us; the launch traced here: 384 us
  loops' own time  154 us (40%)
  starting transfers between devices  59.8 us (15%)
  other arithmetic  50.4 us (13%)
  waiting for transfers between devices  40.1 us (10%)
  blocking collectives  36.7 us (9%)
  local copies, waits for them, and re-layouts  31.1 us (8%)
  matrix products  12.2 us (3%)
    another operation x1, loops' own time, legendre_table(): unused, table_blocks = lax.scan(advance_block, (blank, blank), starts)  154 us
    all_to_all x1, waiting for transfers between devices, shards(): lax.all_to_all(cycle_modes, 'lat', split_axis=0, concat_axis=1, tiled=True)  27.1 us
    while x240, other arithmetic  21 us
    all_to_all x1, blocking collectives, from_everyone(): return lax.all_to_all(copies, axis, split_axis=0, concat_axis=0, tiled=True)  19.9 us
    all_to_all x1, starting transfers between devices, shards(): lax.all_to_all(cycle_modes, 'lat', split_axis=0, concat_axis=1, tiled=True)  18.3 us
    all_to_all x1, starting transfers between devices, shards(): lax.all_to_all(spectrum, 'lat', split_axis=1, concat_axis=0, tiled=True)  16.9 us
    all_to_all x1, blocking collectives, shards(): lax.all_to_all(all_lons.astype(jnp.bfloat16), 'lon', split_axis=1, concat...  16.8 us
    eq x256, other arithmetic, advance_block(): degree == orders[:, None]  11.4 us
  transfers between devices with their start and end apart: 7, of which 3 were waited for; matrix products, arithmetic and copies ran while one was open for 15% of the time, Pallas kernels for 0%

commit v1 on v0

--- a/solution.py
+++ b/solution.py
@@ -3,6 +3,7 @@
 import jax.numpy as jnp
 from jax import lax
 from jax.sharding import PartitionSpec as P
+from jax.lax import all_to_all, axis_size
 
 M = 256
 norm_eps = 1e-06
@@ -188,7 +189,19 @@
     cycle_modes = jnp.einsum(
         "lmt,lmrc->tmrc", synthesis_legendre, mixed, preferred_element_type=jnp.float32
     ).astype(jnp.bfloat16)
-    band_modes = lax.all_to_all(cycle_modes, "lat", split_axis=0, concat_axis=1, tiled=True)
+
+    def yards_choose(mine, dim_no, join_dim):
+        return jnp.concatenate(
+            all_to_all(
+                jnp.stack(jnp.split(mine, axis_size("lat"), axis=dim_no)),
+                axis_name="lat",
+                split_axis=0,
+                concat_axis=0,
+            ),
+            axis=join_dim,
+        )
+
+    band_modes = yards_choose(cycle_modes, 0, 1)
     inverse_table = synthesis_table(jnp.arange(lon_total, dtype=jnp.int32), lon_total, mode_count)
     all_lons = jnp.einsum(
         "tmrc,rmp->tpc", band_modes, inverse_table, preferred_element_type=jnp.float32

time: 387 us -> 533 us (1.38)
  local copies, waits for them, and re-layouts: 31.1 us -> 158 us
  loops' own time: 154 us -> 166 us
    unnamed x19 -> x134, local copies, waits for them, and re-layouts: 1.24 us -> 99.8 us
    another operation x2 -> x4, local copies, waits for them, and re-layouts: 0.27 us -> 19.3 us  [the longest x2 19 us: yards_choose(): jnp.stack(jnp.split(mine, axis_size('lat'), axis=dim_no))]
    another operation x1, loops' own time: 154 us -> 166 us  [legendre_table(): unused, table_blocks = lax.scan(advance_block, (blank, blank), starts)]
    dynamic_update_slice x16, local copies, waits for them, and re-layouts: 0.2 us -> 9.78 us  [legendre_table(): unused, table_blocks = lax.scan(advance_block, (blank, blank), starts)]
  transfers between devices with their start and end apart: 7 -> 7, of which waited for: 3 -> 3; matrix products, arithmetic and copies ran while one was open for 15% -> 13% of each run, Pallas kernels for 0% -> 0%
where the time goes in v1:
time: 533 us; the launch traced here: 529 us
  loops' own time  166 us (31%)
  local copies, waits for them, and re-layouts  158 us (30%)
  starting transfers between devices  60 us (11%)
  other arithmetic  52.2 us (10%)
  waiting for transfers between devices  40.1 us (8%)
  blocking collectives  36.7 us (7%)
  matrix products  15.4 us (3%)
    another operation x1, loops' own time, legendre_table(): unused, table_blocks = lax.scan(advance_block, (blank, blank), starts)  166 us
    unnamed x134, local copies, waits for them, and re-layouts  99.8 us
    all_to_all x1, waiting for transfers between devices, yards_choose(): all_to_all(jnp.stack(jnp.split(mine, axis_size('lat'), axis=dim_no)), axi...  27.1 us
    while x240, other arithmetic  21 us
    all_to_all x1, blocking collectives, from_everyone(): return lax.all_to_all(copies, axis, split_axis=0, concat_axis=0, tiled=True)  19.9 us
    another operation x2, local copies, waits for them, and re-layouts, yards_choose(): jnp.stack(jnp.split(mine, axis_size('lat'), axis=dim_no))  19 us
    all_to_all x1, starting transfers between devices, yards_choose(): all_to_all(jnp.stack(jnp.split(mine, axis_size('lat'), axis=dim_no)), axi...  18.5 us
    all_to_all x1, starting transfers between devices, shards(): lax.all_to_all(spectrum, 'lat', split_axis=1, concat_axis=0, tiled=True)  16.9 us
  transfers between devices with their start and end apart: 7, of which 3 were waited for; matrix products, arithmetic and copies ran while one was open for 13% of the time, Pallas kernels for 0%

profile of v1, /device:TPU:1, one launch (start us, length us, event | category | flops | bytes accessed | tf_op | source)
XLA Modules:
  0.0 529.1 jit_solution(14343557031702392571)
XLA Ops:
  0.0 1.2 copy.345
  1.2 4.5 collective-permute-start
  5.7 6.2 %collective-permute-start.1 = (bf16[2,1,640]{2,1,0:T(2,128)(2,1)S(1)}, bf16[2,1,640]{2,1,0:T(2,128)(2,1)S(1)}, u32[]{:S(2)}, u32[]{:S(2)}) collective-permute-start(bf16[2,1,640]{2,1,0:T(2,128)(2,1)S(1)} %get-tuple-element.534), channel_id=1, source_target_pairs={{1,0},{2,1},{3,2},{0,3},{5,4},{6,5},{7,6},{4,7},{9,8},{10,9},{11,1... | collective-permute-start | bytes 7688 | tf_op jit(solution)/shard_map/ppermute | solution.py:22
  11.9 0.9 slice_reduce_fusion.8
  13.1 2.1 collective-permute-start.2
  15.2 1.3 collective-permute-start.3
  16.5 4.2 sine_negate_fusion
  20.8 3.9 collective-permute-done.3
  24.8 2.1 fusion.67
  27.0 1.8 copy.349
  28.8 10.6 %all-to-all-start = ((bf16[2,180,640]{1,0,2:T(2,128)(2,1)}), bf16[2,180,640]{1,0,2:T(2,128)(2,1)S(1)}, u32[]{:S(2)}, u32[]{:S(2)}) async-start(bf16[2,180,640]{1,0,2:T(2,128)(2,1)} %copy.349), calls=%async_computation | async-start | bytes 1310720 | tf_op jit(solution)/shard_map/all_to_all | solution.py:142
  39.6 9.1 %all-to-all-done = bf16[2,180,640]{1,0,2:T(2,128)(2,1)S(1)} async-done(((bf16[2,180,640]{1,0,2:T(2,128)(2,1)}), bf16[2,180,640]{1,0,2:T(2,128)(2,1)S(1)}, u32[]{:S(2)}, u32[]{:S(2)}) %all-to-all-start) | async-done | bytes 460832 | tf_op jit(solution)/shard_map/all_to_all | solution.py:142
  49.6 1.8 fusion.56
  51.4 1.1 copy.352
  52.5 16.9 %all-to-all-start.1 = ((bf16[2,256,2,160]{3,0,2,1:T(2,128)(2,1)}), bf16[2,256,2,160]{3,0,2,1:T(2,128)(2,1)S(1)}, u32[]{:S(2)}, u32[]{:S(2)}) async-start(bf16[2,256,2,160]{3,0,2,1:T(2,128)(2,1)} %copy.352), calls=%async_computation.1 | async-start | bytes 1048576 | tf_op jit(solution)/shard_map/all_to_all | solution.py:147
  69.4 226.0 %while.21 = (s32[]{:T(128)}, f32[2,256]{1,0:T(2,128)S(1)}, f32[2,256]{1,0:T(2,128)S(1)}, f32[16,16,2,256]{3,2,1,0:T(2,128)}, s32[16]{0:T(128)S(1)}, /*index=5*/s...) while((s32[]{:T(128)}, f32[2,256]{1,0:T(2,128)S(1)}, ...), condition=%wide.region_2.3_spmd.clone.clone.clone.clone, body=%wide.region_1.2_spmd.clone.clone.clone.clone.sunk | while | flops 92737 | bytes 280300 | solution.py:90
  295.4 1.0 slice_bitcast_fusion.129
  296.8 1.4 convolution_bitcast_fusion.1
  298.5 19.9 %all_to_all.55 = bf16[4,256,2,2,160]{1,4,3,2,0:T(8,128)(2,1)S(1)} all-to-all(bf16[4,256,2,2,160]{1,4,3,2,0:T(8,128)(2,1)S(1)} %broadcast_in_dim.453), channel_id=1, replica_groups=mesh['lat'=128,'lon'=4] {'lon'}, dimensions={0} | all-to-all | bytes 2621440 | tf_op jit(solution)/shard_map/all_to_all | solution.py:35
  318.6 1.8 copy.358
  320.4 2.1 reshape_squeeze.6
  322.5 2.0 fusion.112
  324.5 1.3 fusion.108
  325.8 1.3 copy.359
  327.3 1.4 fusion.57
  329.3 1.3 fusion.58
  331.0 1.3 fusion.55
  333.8 0.8 constant_dynamic-update-slice_fusion.141
  339.2 0.8 constant_dynamic-update-slice_fusion.134
  343.1 0.8 constant_dynamic-update-slice_fusion.129
  345.5 0.8 constant_dynamic-update-slice_fusion.126
  355.6 0.8 constant_dynamic-update-slice_fusion.113
  357.1 0.8 constant_dynamic-update-slice_fusion.111
  357.9 0.8 constant_dynamic-update-slice_fusion.110
  361.8 0.8 constant_dynamic-update-slice_fusion.105
  363.4 0.8 constant_dynamic-update-slice_fusion.103
  364.2 0.8 constant_dynamic-update-slice_fusion.102
  368.1 0.8 constant_dynamic-update-slice_fusion.97
  368.8 0.8 constant_dynamic-update-slice_fusion.96
  369.6 0.8 constant_dynamic-update-slice_fusion.95
  379.8 0.8 constant_dynamic-update-slice_fusion.82
  390.6 0.8 constant_dynamic-update-slice_fusion.68
  394.5 0.8 constant_dynamic-update-slice_fusion.63
  400.7 0.8 constant_dynamic-update-slice_fusion.55
  401.5 0.8 constant_dynamic-update-slice_fusion.54
  415.4 0.8 constant_dynamic-update-slice_fusion.36
  417.8 0.8 constant_dynamic-update-slice_fusion.33
  421.6 0.8 constant_dynamic-update-slice_fusion.28
  423.2 0.8 constant_dynamic-update-slice_fusion.26
  426.3 0.8 constant_dynamic-update-slice_fusion.22
  427.9 0.8 constant_dynamic-update-slice_fusion.20
  431.0 0.8 constant_dynamic-update-slice_fusion.16
  431.8 18.2 %copy.365 = bf16[128,2,2,2,160]{4,3,2,1,0:T(2,128)(2,1)} copy(bf16[128,2,2,2,160]{1,4,3,2,0:T(8,128)(2,1)} %constant_dynamic-update-slice_fusion.16) | data formatting | bytes 655360 | tf_op jit(solution)/shard_map/stack | solution.py:196
  450.0 18.5 %all-to-all-start.3 = ((bf16[128,2,2,2,160]{4,3,2,1,0:T(2,128)(2,1)}), bf16[128,2,2,2,160]{4,3,2,1,0:T(2,128)(2,1)S(1)}, u32[]{:S(2)}, u32[]{:S(2)}) async-start(bf16[128,2,2,2,160]{4,3,2,1,0:T(2,128)(2,1)} %copy.365), calls=%async_computation.3 | async-start | bytes 1048576 | tf_op jit(solution)/shard_map/all_to_all | solution.py:195
  468.6 4.1 multiply_convert_fusion.1
  472.6 27.1 %all-to-all-done.3 = bf16[128,2,2,2,160]{4,3,2,1,0:T(2,128)(2,1)S(1)} async-done(((bf16[128,2,2,2,160]{4,3,2,1,0:T(2,128)(2,1)}), bf16[128,2,2,2,160]{4,3,2,1,0:T(2,128)(2,1)S(1)}, u32[]{:S(2)}, u32[]{:S(2)}) %all-to-all-start.3) | async-done | bytes 327712 | tf_op jit(solution)/shard_map/all_to_all | solution.py:195
  500.1 1.5 fusion.54
  501.6 1.0 copy.368
  502.6 16.8 %all_to_all.56 = bf16[2,720,160]{2,0,1:T(2,128)(2,1)S(1)} all-to-all(bf16[2,720,160]{2,0,1:T(2,128)(2,1)S(1)} %copy.368), channel_id=1, replica_groups=mesh['lat'=128,'lon'=4] {'lon'}, dimensions={1} | all-to-all | bytes 921600 | tf_op jit(solution)/shard_map/all_to_all | solution.py:209
  519.7 1.9 reshape.1021
  521.7 1.5 multiply_reduce_fusion
  523.2 1.0 reshape.1018
  524.5 3.4 fusion.53
  528.0 1.1 copy.370
  (967 shorter events, 143.7 us)
Async XLA Ops:
  0.0 524.4 %copy-start = (bf16[1280,640]{1,0:T(8,128)(2,1)S(1)}, bf16[1280,640]{1,0:T(8,128)(2,1)}, u32[]{:S(2)}) copy-start(bf16[1280,640]{1,0:T(8,128)(2,1)} %param.15) | copy-start | bytes 4915204
  1.2 11.7 %collective-permute-start = (bf16[2,1,640]{2,1,0:T(2,128)(2,1)S(1)}, bf16[2,1,640]{2,1,0:T(2,128)(2,1)S(1)}, u32[]{:S(2)}, u32[]{:S(2)}) collective-permute-start(bf16[2,1,640]{2,1,0:T(2,128)(2,1)S(1)} %get-tuple-element.533), channel_id=1, source_target_pairs={{0,1},{1,2},{2,3},{3,0},{4,5},{5,6},{6,7},{7,4},{8,9},{9,10},{10,1... | collective-permute-start | bytes 7688 | tf_op jit(solution)/shard_map/ppermute | solution.py:21
  5.7 7.2 %collective-permute-start.1 = (bf16[2,1,640]{2,1,0:T(2,128)(2,1)S(1)}, bf16[2,1,640]{2,1,0:T(2,128)(2,1)S(1)}, u32[]{:S(2)}, u32[]{:S(2)}) collective-permute-start(bf16[2,1,640]{2,1,0:T(2,128)(2,1)S(1)} %get-tuple-element.534), channel_id=1, source_target_pairs={{1,0},{2,1},{3,2},{0,3},{5,4},{6,5},{7,6},{4,7},{9,8},{10,9},{11,1... | collective-permute-start | bytes 7688 | tf_op jit(solution)/shard_map/ppermute | solution.py:22
  13.1 7.6 %collective-permute-start.2 = (bf16[1,182,640]{2,1,0:T(8,128)(2,1)S(1)}, bf16[1,182,640]{2,1,0:T(8,128)(2,1)S(1)}, u32[]{:S(2)}, u32[]{:S(2)}) collective-permute-start(bf16[1,182,640]{2,1,0:T(8,128)(2,1)S(1)} %get-tuple-element.531), channel_id=1, source_target_pairs={{0,4},{4,8},{8,12},{12,16},{16,20},{20,24},{24,28},{28,32},{32,36}... | collective-permute-start | bytes 698888 | tf_op jit(solution)/shard_map/ppermute | solution.py:21
  15.2 9.5 %collective-permute-start.3 = (bf16[1,182,640]{2,1,0:T(8,128)(2,1)S(1)}, bf16[1,182,640]{2,1,0:T(8,128)(2,1)S(1)}, u32[]{:S(2)}, u32[]{:S(2)}) collective-permute-start(bf16[1,182,640]{2,1,0:T(8,128)(2,1)S(1)} %get-tuple-element.532), channel_id=1, source_target_pairs={{4,0},{8,4},{12,8},{16,12},{20,16},{24,20},{28,24},{32,28},{36,32}... | collective-permute-start | bytes 698888 | tf_op jit(solution)/shard_map/ppermute | solution.py:22
  27.0 42.4 %copy-start.1 = (bf16[2,180,640]{2,1,0:T(8,128)(2,1)}, bf16[2,180,640]{2,1,0:T(8,128)(2,1)S(1)}, u32[]{:S(2)}) copy-start(bf16[2,180,640]{2,1,0:T(8,128)(2,1)S(1)} %fusion.67) | copy-start | bytes 1382404
  28.8 19.8 %all-to-all-start = ((bf16[2,180,640]{1,0,2:T(2,128)(2,1)}), bf16[2,180,640]{1,0,2:T(2,128)(2,1)S(1)}, u32[]{:S(2)}, u32[]{:S(2)}) async-start(bf16[2,180,640]{1,0,2:T(2,128)(2,1)} %copy.349), calls=%async_computation | async-start | bytes 1310720 | tf_op jit(solution)/shard_map/all_to_all | solution.py:142
  52.5 243.9 %all-to-all-start.1 = ((bf16[2,256,2,160]{3,0,2,1:T(2,128)(2,1)}), bf16[2,256,2,160]{3,0,2,1:T(2,128)(2,1)S(1)}, u32[]{:S(2)}, u32[]{:S(2)}) async-start(bf16[2,256,2,160]{3,0,2,1:T(2,128)(2,1)} %copy.352), calls=%async_computation.1 | async-start | bytes 1048576 | tf_op jit(solution)/shard_map/all_to_all | solution.py:147
  423.2 101.0 %copy-start.2 = (f32[640]{0:T(1024)S(1)}, f32[640]{0:T(1024)}, u32[]{:S(2)}) copy-start(f32[640]{0:T(1024)} %param.13) | copy-start | bytes 7684
  450.0 49.8 %all-to-all-start.3 = ((bf16[128,2,2,2,160]{4,3,2,1,0:T(2,128)(2,1)}), bf16[128,2,2,2,160]{4,3,2,1,0:T(2,128)(2,1)S(1)}, u32[]{:S(2)}, u32[]{:S(2)}) async-start(bf16[128,2,2,2,160]{4,3,2,1,0:T(2,128)(2,1)} %copy.365), calls=%async_computation.3 | async-start | bytes 1048576 | tf_op jit(solution)/shard_map/all_to_all | solution.py:195
